TPU v7x, 32 devices: a whole 2x2x4 slice. The times are simulated.
32 devices in a mesh: dp: 8 (over z, core), tensor: 4 (over y, x).
Axes of the slice: x: 2, y: 2, z: 4, core: 2. Of those that a mesh axis runs over, the one named last changes fastest.
Arguments:
- block_input: bfloat16 [16, 736, 1152], P('dp', 'tensor'), may hold values from -40 to 40
- key_mask: int32 [16, 736], P('dp'), may hold values from 0 to 1, as said below
- attn_norm_gain: float32 [1152], replicated, may hold values from 0.5 to 1.5
- attn_norm_bias: float32 [1152], replicated, may hold values from -1.5 to 1.5
- qkv_weight: bfloat16 [1152, 3, 1152], P('dp', None, 'tensor'), may hold values from -1.5 to 1.5
- qv_bias: float32 [2, 1152], P(None, 'tensor'), may hold values from -2.5 to 2.5
- out_weight: bfloat16 [1152, 1152], P('tensor', 'dp'), may hold values from -0.5 to 0.5
- out_bias: float32 [1152], replicated, may hold values from -2.5 to 2.5
- mlp_norm_gain: float32 [1152], replicated, may hold values from 0.5 to 1.5
- mlp_norm_bias: float32 [1152], replicated, may hold values from -1.5 to 1.5
- hidden_weight: bfloat16 [1152, 4304], P('dp', 'tensor'), may hold values from -0.1875 to 0.1875
- hidden_bias: float32 [4304], P('tensor'), may hold values from -2.5 to 2.5
- down_weight: bfloat16 [4304, 1152], P('tensor', 'dp'), may hold values from -0.125 to 0.125
- down_bias: float32 [1152], replicated, may hold values from -2.5 to 2.5
- grad_out: bfloat16 [16, 736, 1152], P('dp', 'tensor'), may hold values from -6 to 6
Outputs:
- block_output: bfloat16 [16, 736, 1152], P('dp', 'tensor')
- grad_input: float32 [16, 736, 1152], P('dp', 'tensor')
- grad_attn_norm_gain: float32 [1152], replicated
- grad_attn_norm_bias: float32 [1152], replicated
- grad_qkv_weight: float32 [1152, 3, 1152], P('dp', None, 'tensor')
- grad_qv_bias: float32 [2, 1152], P(None, 'tensor')
- grad_out_weight: float32 [1152, 1152], P('tensor', 'dp')
- grad_out_bias: float32 [1152], replicated
- grad_mlp_norm_gain: float32 [1152], replicated
- grad_mlp_norm_bias: float32 [1152], replicated
- grad_hidden_weight: float32 [1152, 4304], P('dp', 'tensor')
- grad_hidden_bias: float32 [4304], P('tensor')
- grad_down_weight: float32 [4304, 1152], P('tensor', 'dp')
- grad_down_bias: float32 [1152], replicated
Inputs may be any that keep to these rules, and one draw needn't show every extreme that they name: `key_mask`: each image's mask is 1 on its first L positions and 0 after them, with L from 368 to 729; some image has L = 729.
All inputs are finite; a program needn't handle non-finite values.
Results may differ from a plain program's by a relative error of at most 0.0095.
The roundings to bfloat16 on the way count: a program that leaves them out, or rounds other values in their place, can miss the bound.
Values may be sent and summed in bfloat16 or wider, within the bound.
A program may use at most 192 MiB of HBM per device.

v0:
```python
import math

import jax
import jax.numpy as jnp
from jax import lax
from jax.sharding import PartitionSpec as P

HD = 72


layer_eps = 1e-06
gelu_root = math.sqrt(2.0 / math.pi)
gelu_cubic = 0.044715


def norm_forward(rows, gain, shift):
    center = rows - jnp.mean(rows, axis=-1, keepdims=True)
    inv_std = lax.rsqrt(jnp.mean(center * center, axis=-1, keepdims=True) + layer_eps)
    unit = center * inv_std
    return ((unit * gain + shift).astype(jnp.bfloat16), unit, inv_std)


def norm_backward(grad_normed, unit, inv_std, gain):
    scaled = grad_normed * gain
    return inv_std * (
        scaled
        - jnp.mean(scaled, axis=-1, keepdims=True)
        - unit * jnp.mean(scaled * unit, axis=-1, keepdims=True)
    )


def gelu_forward(pre):
    inner = gelu_root * (pre + gelu_cubic * pre * pre * pre)
    return 0.5 * pre * (1.0 + jnp.tanh(inner))


def gelu_slope(pre):
    tangent = jnp.tanh(gelu_root * (pre + gelu_cubic * pre * pre * pre))
    return 0.5 * (1.0 + tangent) + 0.5 * pre * (1.0 - tangent * tangent) * gelu_root * (
        1.0 + 3.0 * gelu_cubic * pre * pre
    )


def score_block(queries, keys_in, valid):
    scale = queries.shape[-1] ** (-0.5)
    scores = (
        jnp.einsum("qhd,khd->hqk", queries, keys_in, preferred_element_type=jnp.float32) * scale
    )
    return jnp.where(valid[None, None, :] > 0, scores, -1e30)


def attend_forward(packed):
    queries, keys_in, values, valid = packed
    scores = score_block(queries, keys_in, valid)
    top = jnp.max(scores, axis=-1, keepdims=True)
    log_total = top + jnp.log(jnp.sum(jnp.exp(scores - top), axis=-1, keepdims=True))
    weights = jnp.exp(scores - log_total).astype(jnp.bfloat16)
    mixed = jnp.einsum("hqk,khd->qhd", weights, values, preferred_element_type=jnp.float32).astype(
        jnp.bfloat16
    )
    return (mixed, log_total)


def attend_backward(packed):
    queries, keys_in, values, grad_mixed, log_total, valid = packed
    scale = queries.shape[-1] ** (-0.5)
    probs = jnp.exp(score_block(queries, keys_in, valid) - log_total)
    weights = probs.astype(jnp.bfloat16)
    grad_probs = jnp.einsum("qhd,khd->hqk", grad_mixed, values, preferred_element_type=jnp.float32)
    delta = jnp.sum(probs * grad_probs, axis=-1, keepdims=True)
    grad_scores = (probs * (grad_probs - delta) * scale).astype(jnp.bfloat16)
    grad_queries = jnp.einsum(
        "hqk,khd->qhd", grad_scores, keys_in, preferred_element_type=jnp.float32
    )
    grad_keys = jnp.einsum("hqk,qhd->khd", grad_scores, queries, preferred_element_type=jnp.float32)
    grad_values = jnp.einsum(
        "hqk,qhd->khd", weights, grad_mixed, preferred_element_type=jnp.float32
    )
    return (grad_queries, grad_keys, grad_values)


def shards(
    block_input,
    key_mask,
    attn_norm_gain,
    attn_norm_bias,
    qkv_weight,
    qv_bias,
    out_weight,
    out_bias,
    mlp_norm_gain,
    mlp_norm_bias,
    hidden_weight,
    hidden_bias,
    down_weight,
    down_bias,
    grad_out,
):
    qkv_all, out_all, hidden_all, down_all = (
        lax.all_gather(qkv_weight, "dp", axis=0, tiled=True),
        lax.all_gather(out_weight, "dp", axis=1, tiled=True),
        lax.all_gather(hidden_weight, "dp", axis=0, tiled=True),
        lax.all_gather(down_weight, "dp", axis=1, tiled=True),
    )
    images, seq_full = key_mask.shape
    width_local = qkv_all.shape[2]
    head_dim = HD
    heads_local = width_local // head_dim
    in_float = block_input.astype(jnp.float32)
    normed_one, unit_one, inv_one = norm_forward(in_float, attn_norm_gain, attn_norm_bias)
    gathered_one = lax.all_gather(normed_one, "tensor", axis=1, tiled=True)
    projected = jnp.einsum(
        "isd,dcf->iscf", gathered_one, qkv_all, preferred_element_type=jnp.float32
    )
    head_shape = (images, seq_full, heads_local, head_dim)
    queries = (projected[:, :, 0] + qv_bias[0]).astype(jnp.bfloat16).reshape(head_shape)
    keys_in = projected[:, :, 1].astype(jnp.bfloat16).reshape(head_shape)
    values = (projected[:, :, 2] + qv_bias[1]).astype(jnp.bfloat16).reshape(head_shape)
    mixed, log_total = lax.map(attend_forward, (queries, keys_in, values, key_mask))
    mixed_flat = mixed.reshape(images, seq_full, width_local)
    attn_part = jnp.einsum("isf,fd->isd", mixed_flat, out_all, preferred_element_type=jnp.float32)
    attn_sum = lax.psum_scatter(attn_part, "tensor", scatter_dimension=1, tiled=True)
    hidden_res = in_float + attn_sum + out_bias
    normed_two, unit_two, inv_two = norm_forward(hidden_res, mlp_norm_gain, mlp_norm_bias)
    gathered_two = lax.all_gather(normed_two, "tensor", axis=1, tiled=True)
    pre_act = (
        jnp.einsum("isd,df->isf", gathered_two, hidden_all, preferred_element_type=jnp.float32)
        + hidden_bias
    )
    activated = gelu_forward(pre_act).astype(jnp.bfloat16)
    mlp_part = jnp.einsum("isf,fd->isd", activated, down_all, preferred_element_type=jnp.float32)
    mlp_sum = lax.psum_scatter(mlp_part, "tensor", scatter_dimension=1, tiled=True)
    block_output = (hidden_res + mlp_sum + down_bias).astype(jnp.bfloat16)
    grad_float = grad_out.astype(jnp.float32)
    grad_full = lax.all_gather(grad_out, "tensor", axis=1, tiled=True)
    grad_down_w = jnp.einsum(
        "isf,isd->fd", activated, grad_full, preferred_element_type=jnp.float32
    )
    grad_down_b = jnp.sum(grad_float, axis=(0, 1))
    grad_act = jnp.einsum("isd,fd->isf", grad_full, down_all, preferred_element_type=jnp.float32)
    grad_pre = grad_act * gelu_slope(pre_act)
    grad_hidden_b = jnp.sum(grad_pre, axis=(0, 1))
    grad_pre_low = grad_pre.astype(jnp.bfloat16)
    used_two = lax.all_gather(normed_two, "tensor", axis=1, tiled=True)
    grad_hidden_w = jnp.einsum(
        "isd,isf->df", used_two, grad_pre_low, preferred_element_type=jnp.float32
    )
    normed_two_part = jnp.einsum(
        "isf,df->isd", grad_pre_low, hidden_all, preferred_element_type=jnp.float32
    )
    grad_normed_two = lax.psum_scatter(normed_two_part, "tensor", scatter_dimension=1, tiled=True)
    grad_mlp_gain = jnp.sum(grad_normed_two * unit_two, axis=(0, 1))
    grad_mlp_shift = jnp.sum(grad_normed_two, axis=(0, 1))
    grad_hidden = grad_float + norm_backward(grad_normed_two, unit_two, inv_two, mlp_norm_gain)
    grad_out_b = jnp.sum(grad_hidden, axis=(0, 1))
    grad_hidden_low = grad_hidden.astype(jnp.bfloat16)
    hidden_full = lax.all_gather(grad_hidden_low, "tensor", axis=1, tiled=True)
    grad_out_w = jnp.einsum(
        "isf,isd->fd", mixed_flat, hidden_full, preferred_element_type=jnp.float32
    )
    grad_mixed = (
        jnp.einsum("isd,fd->isf", hidden_full, out_all, preferred_element_type=jnp.float32)
        .astype(jnp.bfloat16)
        .reshape(head_shape)
    )
    grad_queries, grad_keys, grad_values = lax.map(
        attend_backward, (queries, keys_in, values, grad_mixed, log_total, key_mask)
    )
    flat_shape = (images, seq_full, width_local)
    grad_queries = grad_queries.reshape(flat_shape)
    grad_keys = grad_keys.reshape(flat_shape)
    grad_values = grad_values.reshape(flat_shape)
    grad_qv_b = jnp.stack([jnp.sum(grad_queries, axis=(0, 1)), jnp.sum(grad_values, axis=(0, 1))])
    grad_projected = jnp.stack([grad_queries, grad_keys, grad_values], axis=2).astype(jnp.bfloat16)
    used_one = lax.all_gather(normed_one, "tensor", axis=1, tiled=True)
    grad_qkv_w = jnp.einsum(
        "isd,iscf->dcf", used_one, grad_projected, preferred_element_type=jnp.float32
    )
    normed_one_part = jnp.einsum(
        "iscf,dcf->isd", grad_projected, qkv_all, preferred_element_type=jnp.float32
    )
    grad_normed_one = lax.psum_scatter(normed_one_part, "tensor", scatter_dimension=1, tiled=True)
    grad_attn_gain = jnp.sum(grad_normed_one * unit_one, axis=(0, 1))
    grad_attn_shift = jnp.sum(grad_normed_one, axis=(0, 1))
    grad_input = grad_hidden + norm_backward(grad_normed_one, unit_one, inv_one, attn_norm_gain)
    owned_qkv, owned_out, owned_hidden, owned_down = (
        lax.psum_scatter(grad_qkv_w, "dp", scatter_dimension=0, tiled=True),
        lax.psum_scatter(grad_out_w, "dp", scatter_dimension=1, tiled=True),
        lax.psum_scatter(grad_hidden_w, "dp", scatter_dimension=0, tiled=True),
        lax.psum_scatter(grad_down_w, "dp", scatter_dimension=1, tiled=True),
    )
    summed_qv, summed_hidden_b = lax.psum((grad_qv_b, grad_hidden_b), "dp")
    (
        total_attn_gain,
        total_attn_shift,
        total_out_b,
        total_mlp_gain,
        total_mlp_shift,
        total_down_b,
    ) = lax.psum(
        (grad_attn_gain, grad_attn_shift, grad_out_b, grad_mlp_gain, grad_mlp_shift, grad_down_b),
        ("dp", "tensor"),
    )
    return (
        block_output,
        grad_input,
        total_attn_gain,
        total_attn_shift,
        owned_qkv,
        summed_qv,
        owned_out,
        total_out_b,
        total_mlp_gain,
        total_mlp_shift,
        owned_hidden,
        summed_hidden_b,
        owned_down,
        total_down_b,
    )


def solution(mesh):
    return jax.shard_map(
        shards,
        mesh=mesh,
        in_specs=(
            P("dp", "tensor", None),
            P("dp", None),
            P(),
            P(),
            P("dp", None, "tensor"),
            P(None, "tensor"),
            P("tensor", "dp"),
            P(),
            P(),
            P(),
            P("dp", "tensor"),
            P("tensor"),
            P("tensor", "dp"),
            P(),
            P("dp", "tensor", None),
        ),
        out_specs=(
            P("dp", "tensor", None),
            P("dp", "tensor", None),
            P(),
            P(),
            P("dp", None, "tensor"),
            P(None, "tensor"),
            P("tensor", "dp"),
            P(),
            P(),
            P(),
            P("dp", "tensor"),
            P("tensor"),
            P("tensor", "dp"),
            P(),
        ),
        check_vma=False,
    )
```

profile of v0, /device:TPU:0, one launch (start us, length us, event | category | flops | bytes accessed | tf_op | source)
XLA Modules:
  0.0 1009.4 jit_solution(3070976743139038333)
XLA Ops:
  8.0 1.3 convert_reduce_fusion
  9.3 1.5 fusion.129
  10.9 2.5 fusion.123
  13.6 23.4 %all_gather.28 = bf16[288,1152]{0,1:T(8,128)(2,1)S(1)} all-gather(bf16[288,144]{0,1:T(8,128)(2,1)S(1)} %copy-done.12), channel_id=1, replica_groups=mesh['dp'=8,'tensor'=4] {'dp'}, dimensions={1}, use_global_device_ids=true | all-gather | bytes 746496 | tf_op jit(solution)/shard_map/all_gather | solution.py:101
  37.0 13.4 %all-gather.10.cloned.1.call-done = bf16[1152,3,288]{2,0,1:T(8,128)(2,1)} async-done(((bf16[144,3,288]{2,0,1:T(8,128)(2,1)}), bf16[1152,3,288]{2,0,1:T(8,128)(2,1)}) %all-gather.10.cloned.1.call-update) | async-done | bytes 1990672 | tf_op jit(solution)/shard_map/all_gather | solution.py:100
  50.4 48.7 %all-gather.8.cloned.1.call-done = bf16[2,736,1152]{2,1,0:T(8,128)(2,1)} async-done(((bf16[2,184,1152]{2,1,0:T(8,128)(2,1)}), bf16[2,736,1152]{2,1,0:T(8,128)(2,1)}) %all-gather.8.cloned.1.call-update) | async-done | bytes 3391504 | tf_op jit(solution)/shard_map/all_gather | solution.py:111
  99.1 6.6 fusion.105
  106.4 16.9 %while.26 = (s32[]{:T(128)}, bf16[2,736,4,72]{1,3,2,0:T(8,128)(2,1)}, f32[2,4,736,1]{2,1,3,0:T(4,128)}, bf16[2,736,4,72]{1,3,2,0:T(8,128)(2,1)S(1)}, s32[2,736]{...) while((s32[]{:T(128)}, ...), condition=%wide.region_5.6_spmd, body=%wide.region_2.5_spmd.sunk | while | flops 648078208 | bytes 35224596 | solution.py:119
  107.4 2.1 fusion.174
  109.5 2.3 exponential_reduce_fusion.2
  111.8 2.2 fusion.175
  114.0 0.9 copy-done.8
  115.7 2.1 fusion.174
  117.8 2.3 exponential_reduce_fusion.2
  120.1 2.2 fusion.175
  122.3 0.9 copy-done.8
  123.2 6.4 fusion.134
  130.4 74.2 %reduce-scatter.9.cloned.1.call-done = f32[2,184,1152]{2,1,0:T(8,128)} async-done(((f32[2,736,1152]{2,1,0:T(8,128)}), f32[2,184,1152]{2,1,0:T(8,128)}) %reduce-scatter.9.cloned.1.call-update) | async-done | bytes 1695760 | tf_op jit(solution)/shard_map/reduce_scatter | solution.py:122
  204.6 2.0 fusion.139
  206.9 1.3 add_convert_fusion.3
  210.2 29.9 %all-gather.14.cloned.1.call-done = bf16[1152,1076]{1,0:T(8,128)(2,1)} async-done(((bf16[144,1076]{1,0:T(8,128)(2,1)}), bf16[1152,1076]{1,0:T(8,128)(2,1)}) %all-gather.14.cloned.1.call-update) | async-done | bytes 2479120 | tf_op jit(solution)/shard_map/all_gather | solution.py:102
  240.1 47.3 %all-gather.12.cloned.1.call-done = bf16[2,736,1152]{2,1,0:T(8,128)(2,1)} async-done(((bf16[2,184,1152]{2,1,0:T(8,128)(2,1)}), bf16[2,736,1152]{2,1,0:T(8,128)(2,1)}) %all-gather.12.cloned.1.call-update) | async-done | bytes 3391504 | tf_op jit(solution)/shard_map/all_gather | solution.py:125
  287.4 10.1 fusion.112
  297.5 25.4 %all-gather.16.cloned.1.call-done = bf16[1076,1152]{0,1:T(8,128)(2,1)} async-done(((bf16[1076,144]{0,1:T(8,128)(2,1)}), bf16[1076,1152]{0,1:T(8,128)(2,1)}) %all-gather.16.cloned.1.call-update) | async-done | bytes 2479120 | tf_op jit(solution)/shard_map/all_gather | solution.py:103
  322.9 46.9 %all-gather.18.cloned.1.call-done = bf16[2,736,1152]{2,1,0:T(8,128)(2,1)} async-done(((bf16[2,184,1152]{2,1,0:T(8,128)(2,1)}), bf16[2,736,1152]{2,1,0:T(8,128)(2,1)}) %all-gather.18.cloned.1.call-update) | async-done | bytes 3391504 | tf_op jit(solution)/shard_map/all_gather | solution.py:135
  369.8 13.2 %fusion.144 = (f32[1076]{0:T(1024)}, bf16[2,736,1076]{1,2,0:T(8,128)(2,1)S(1)}) fusion(f32[2,736,1076]{1,2,0:T(8,128)} %fusion.112, f32[1076]{0:T(1024)S(1)} %copy-done.30, bf16[2,736,1152]{2,1,0:T(8,128)(2,1)} %all-gather.18.cloned.1.call-done, bf16[1076,1152]{0,1:T(8,128)(2,1)} %all-gather.16.cloned.1.call-done), kind=kOutput, calls=%fused_computation.160 | convolution fusion | flops 3682501376 | bytes 15382432 | tf_op jit(solution)/shard_map/isd,fd->isf/dot_general | solution.py:140
  383.0 1.7 copy-done.33
  384.7 7.1 fusion.110
  392.0 11.9 %fusion.108 = f32[2,736,1152]{2,1,0:T(8,128)} fusion(bf16[1076,1152]{0,1:T(8,128)(2,1)} %all-gather.16.cloned.1.call-done, f32[2,736,1076]{1,2,0:T(8,128)} %fusion.112, f32[1076]{0:T(1024)S(1)} %copy-done.30), kind=kOutput, calls=%fused_computation.97 | convolution fusion | flops 3665079808 | bytes 15601872 | tf_op jit(solution)/shard_map/isf,fd->isd/dot_general | solution.py:131
  404.0 62.7 %reduce-scatter.13.cloned.1.call-done = f32[2,184,1152]{2,1,0:T(8,128)} async-done(((f32[2,736,1152]{2,1,0:T(8,128)}), f32[2,184,1152]{2,1,0:T(8,128)}) %reduce-scatter.13.cloned.1.call-update) | async-done | bytes 1695760 | tf_op jit(solution)/shard_map/reduce_scatter | solution.py:151
  466.7 2.8 multiply_reduce_fusion.1
  469.5 75.0 %reduce-scatter.11.cloned.1.call-done = f32[2,184,1152]{2,1,0:T(8,128)} async-done(((f32[2,736,1152]{2,1,0:T(8,128)}), f32[2,184,1152]{2,1,0:T(8,128)}) %reduce-scatter.11.cloned.1.call-update) | async-done | bytes 1695760 | tf_op jit(solution)/shard_map/reduce_scatter | solution.py:132
  544.5 4.6 fusion.138
  549.1 1.2 copy-done.2
  550.3 1.0 convert_element_type.66
  551.4 46.0 %all-gather.20.cloned.1.call-done = bf16[2,736,1152]{2,1,0:T(8,128)(2,1)} async-done(((bf16[2,184,1152]{2,1,0:T(8,128)(2,1)}), bf16[2,736,1152]{2,1,0:T(8,128)(2,1)}) %all-gather.20.cloned.1.call-update) | async-done | bytes 3391504 | tf_op jit(solution)/shard_map/all_gather | solution.py:157
  597.4 3.5 convolution_convert_fusion
  600.9 91.8 %while.27 = (s32[]{:T(128)}, f32[2,736,4,72]{1,3,2,0:T(8,128)}, bf16[2,736,4,72]{1,3,2,0:T(8,128)(2,1)}, f32[2,736,4,72]{1,3,2,0:T(8,128)}, bf16[2,736,4,72]{1,3...) while((s32[]{:T(128)}, f32[2,736,4,72]{1,3,2,0:T(8,128)}, ...), condition=%wide.region_15.16_spmd, body=%wide.region_13.15_spmd.sunk | while | flops 1616429056 | bytes 139211536 | solution.py:166
  602.4 1.4 fusion.187
  603.8 3.7 fusion.190
  607.4 4.8 fusion.186
  612.2 17.3 %fusion.189 = bf16[2,736,4,72]{1,3,2,0:T(8,128)(2,1)} fusion(bf16[2,736,4,72]{1,3,2,0:T(8,128)(2,1)} %get-tuple-element.334, s32[]{:T(128)S(6)} %copy.59, f32[4,736,736]{1,2,0:T(8,128)} %fusion.186, f32[4,736,736]{1,2,0:T(8,128)} %copy-done, f32[4,736]{1,0:T(4,128)S(1)} %dynamic-slice_bitcast_fusion.2, pred[736]{0:T(1024)(128)(4,1)S(1)} %compare_reduce_fusion.5, ...), kind=kOutput, calls=%fused_computation.46.clone.1 | convolution fusion | flops 335855200 | bytes 37493760 | tf_op jit(solution)/shard_map/while/body/eval_jaxpr/hqk,qhd->khd/dot_general | solution.py:75
  629.5 17.3 %fusion.188 = f32[2,736,4,72]{1,3,2,0:T(8,128)} fusion(f32[2,736,4,72]{1,3,2,0:T(8,128)} %get-tuple-element.333, s32[]{:T(128)S(6)} %copy.59, f32[4,736,736]{1,2,0:T(8,128)} %fusion.186, f32[4,736,736]{1,2,0:T(8,128)} %copy-done, f32[4,736]{1,0:T(4,128)S(1)} %dynamic-slice_bitcast_fusion.2, pred[736]{0:T(1024)(128)(4,1)S(1)} %compare_reduce_fusion.5, ...), kind=kOutput, calls=%fused_computation.44.clone.1 | convolution fusion | flops 335855200 | bytes 37530624 | tf_op jit(solution)/shard_map/while/body/eval_jaxpr/hqk,khd->qhd/dot_general | solution.py:72
  648.2 1.4 fusion.187
  649.6 3.8 fusion.190
  653.4 4.8 fusion.186
  658.2 17.3 %fusion.189 = bf16[2,736,4,72]{1,3,2,0:T(8,128)(2,1)} fusion(bf16[2,736,4,72]{1,3,2,0:T(8,128)(2,1)} %get-tuple-element.334, s32[]{:T(128)S(6)} %copy.59, f32[4,736,736]{1,2,0:T(8,128)} %fusion.186, f32[4,736,736]{1,2,0:T(8,128)} %copy-done, f32[4,736]{1,0:T(4,128)S(1)} %dynamic-slice_bitcast_fusion.2, pred[736]{0:T(1024)(128)(4,1)S(1)} %compare_reduce_fusion.5, ...), kind=kOutput, calls=%fused_computation.46.clone.1 | convolution fusion | flops 335855200 | bytes 37493760 | tf_op jit(solution)/shard_map/while/body/eval_jaxpr/hqk,qhd->khd/dot_general | solution.py:75
  675.4 17.3 %fusion.188 = f32[2,736,4,72]{1,3,2,0:T(8,128)} fusion(f32[2,736,4,72]{1,3,2,0:T(8,128)} %get-tuple-element.333, s32[]{:T(128)S(6)} %copy.59, f32[4,736,736]{1,2,0:T(8,128)} %fusion.186, f32[4,736,736]{1,2,0:T(8,128)} %copy-done, f32[4,736]{1,0:T(4,128)S(1)} %dynamic-slice_bitcast_fusion.2, pred[736]{0:T(1024)(128)(4,1)S(1)} %compare_reduce_fusion.5, ...), kind=kOutput, calls=%fused_computation.44.clone.1 | convolution fusion | flops 335855200 | bytes 37530624 | tf_op jit(solution)/shard_map/while/body/eval_jaxpr/hqk,khd->qhd/dot_general | solution.py:72
  692.8 3.6 fusion.142
  696.8 7.3 convolution_bitcast_fusion.2
  704.2 10.1 %convolution_bitcast_fusion.1 = f32[1152,1076]{1,0:T(8,128)} fusion(bf16[2,736,1152]{2,1,0:T(8,128)(2,1)} %all-gather.12.cloned.1.call-done, bf16[2,736,1076]{1,2,0:T(8,128)(2,1)} %copy-done.33), kind=kOutput, calls=%fused_computation.81 | convolution fusion | flops 3649241088 | bytes 11517440 | tf_op jit(solution)/shard_map/isd,isf->df/dot_general | solution.py:145
  715.0 11.4 %convolution_bitcast_fusion = f32[1076,1152]{0,1:T(8,128)} fusion(bf16[2,736,1152]{2,1,0:T(8,128)(2,1)} %all-gather.18.cloned.1.call-done, f32[2,736,1076]{1,2,0:T(8,128)} %fusion.112, f32[1076]{0:T(1024)S(1)} %copy-done.31), kind=kOutput, calls=%fused_computation.80 | convolution fusion | flops 3665079808 | bytes 14689488 | tf_op jit(solution)/shard_map/isf,isd->fd/dot_general | solution.py:136
  726.5 1.3 copy-done.9
  727.8 5.3 convolution_bitcast_fusion.4
  733.4 9.4 convolution_bitcast_fusion.3
  743.5 28.4 %all-reduce.1 = (f32[2,288]{1,0:T(2,128)}, f32[1076]{0:T(1024)}) all-reduce(f32[2,288]{1,0:T(2,128)S(1)} %pad_maximum_fusion.3, f32[1076]{0:T(1024)S(1)} %copy-done.25), channel_id=1, replica_groups=mesh['dp'=8,'tensor'=4] {'dp'}, use_global_device_ids=true, to_apply=%region_26.27 | all-reduce | flops 1652 | bytes 13216 | tf_op jit(solution)/shard_map/psum | solution.py:192
  771.9 7.2 reduce-scatter.15.cloned.1.call-done
  779.1 2.3 fusion.128
  781.4 42.2 %all-reduce = (f32[1152]{0:T(1024)}, f32[1152]{0:T(1024)}, f32[1152]{0:T(1024)}, f32[1152]{0:T(1024)}, f32[1152]{0:T(1024)}, /*index=5*/f32[1152]{0:T(1024)}) all-reduce(f32[1152]{0:T(1024)S(1)} %get-tuple-element.113, f32[1152]{0:T(1024)S(1)} %get-tuple-element.118, ...), channel_id=1, replica_groups=mesh['dp'=8,'tensor'=4] {'dp','tensor'}, use_global_device_ids=true, to_apply=%region_20.21 | all-reduce | flops 6912 | bytes 55296 | tf_op jit(solution)/shard_map/psum | solution.py:200
  823.5 3.2 fusion.127
  826.8 16.6 %reduce-scatter.21.cloned.1.call-done = f32[144,1076]{1,0:T(8,128)} async-done(((f32[1152,1076]{1,0:T(8,128)}), f32[144,1076]{1,0:T(8,128)}) %reduce-scatter.21.cloned.1.call-update) | async-done | bytes 619792 | tf_op jit(solution)/shard_map/reduce_scatter | solution.py:189
  843.3 61.8 %reduce-scatter.23.cloned.1.call-done = f32[1076,144]{0,1:T(8,128)} async-done(((f32[1076,1152]{0,1:T(8,128)}), f32[1076,144]{0,1:T(8,128)}) %reduce-scatter.23.cloned.1.call-update) | async-done | bytes 619792 | tf_op jit(solution)/shard_map/reduce_scatter | solution.py:190
  905.1 36.5 %reduce-scatter.19.cloned.1.call-done = f32[288,144]{0,1:T(8,128)} async-done(((f32[288,1152]{0,1:T(8,128)}), f32[288,144]{0,1:T(8,128)}) %reduce-scatter.19.cloned.1.call-update) | async-done | bytes 165904 | tf_op jit(solution)/shard_map/reduce_scatter | solution.py:188
  941.6 61.0 %reduce-scatter.17.cloned.1.call-done = f32[144,3,288]{2,0,1:T(8,128)} async-done(((f32[1152,3,288]{2,0,1:T(8,128)}), f32[144,3,288]{2,0,1:T(8,128)}) %reduce-scatter.17.cloned.1.call-update) | async-done | bytes 497680 | tf_op jit(solution)/shard_map/reduce_scatter | solution.py:187
  (135 shorter events, 11.5 us)
Async XLA Ops:
  7.2 6.3 copy-start.27
  7.2 6.5 copy-start.12
  7.2 43.2 %all-gather.10.cloned.1.call-start = ((), (), s32[]{:S(2)}) async-start(), calls=%async_computation.9 | async-start | bytes 2985984 | tf_op jit(solution)/shard_map/all_gather | solution.py:100
  7.9 91.2 %all-gather.8.cloned.1.call-start = ((), (), s32[]{:S(2)}) async-start(), calls=%async_computation.8 | async-start | bytes 4239360 | tf_op jit(solution)/shard_map/all_gather | solution.py:111
  9.3 89.8 %copy-start.15 = (f32[2,184]{1,0:T(2,128)}, f32[2,184]{1,0:T(2,128)S(1)}, u32[]{:S(2)}) copy-start(f32[2,184]{1,0:T(2,128)S(1)} %broadcast_multiply_fusion.5) | copy-start | bytes 4420
  10.9 88.2 %copy-start.17 = (f32[2,184]{1,0:T(2,128)}, f32[2,184]{1,0:T(2,128)S(1)}, u32[]{:S(2)}) copy-start(f32[2,184]{1,0:T(2,128)S(1)} %add_rsqrt_fusion.1) | copy-start | bytes 4420
  13.4 191.2 %reduce-scatter.9.cloned.1.call-start = ((), (), s32[]{:S(2)}) async-start(), calls=%async_computation.10 | async-start | bytes 8478720 | tf_op jit(solution)/shard_map/reduce_scatter | solution.py:122
  37.0 86.2 %copy-start.6 = (bf16[288,1152]{0,1:T(8,128)(2,1)}, bf16[288,1152]{0,1:T(8,128)(2,1)S(1)}, u32[]{:S(2)}) copy-start(bf16[288,1152]{0,1:T(8,128)(2,1)S(1)} %all_gather.28) | copy-start | bytes 1990660
  109.5 2.3 copy-start.10
  109.5 2.3 copy-start.7
  111.8 2.2 copy-start.11
  114.0 0.9 copy-start.8
  117.8 2.3 copy-start.10
  117.8 2.3 copy-start.7
  120.1 2.2 copy-start.11
  122.3 0.9 copy-start.8
  123.2 6.4 copy-start.4
  129.7 74.9 %copy-start.23 = (f32[1152]{0:T(1024)S(1)}, f32[1152]{0:T(1024)}, u32[]{:S(2)}) copy-start(f32[1152]{0:T(1024)} %param.26) | copy-start | bytes 13828
  129.7 77.2 %copy-start.14 = (f32[1152]{0:T(1024)S(1)}, f32[1152]{0:T(1024)}, u32[]{:S(2)}) copy-start(f32[1152]{0:T(1024)} %param.27) | copy-start | bytes 13828
  129.7 77.2 %copy-start.24 = (f32[1152]{0:T(1024)S(1)}, f32[1152]{0:T(1024)}, u32[]{:S(2)}) copy-start(f32[1152]{0:T(1024)} %param.28) | copy-start | bytes 13828
  129.7 110.4 %all-gather.14.cloned.1.call-start = ((), (), s32[]{:S(2)}) async-start(), calls=%async_computation.12 | async-start | bytes 2985984 | tf_op jit(solution)/shard_map/all_gather | solution.py:102
  130.3 157.1 %all-gather.12.cloned.1.call-start = ((), (), s32[]{:S(2)}) async-start(), calls=%async_computation.11 | async-start | bytes 4239360 | tf_op jit(solution)/shard_map/all_gather | solution.py:125
  208.2 114.7 %all-gather.16.cloned.1.call-start = ((), (), s32[]{:S(2)}) async-start(), calls=%async_computation.13 | async-start | bytes 2985984 | tf_op jit(solution)/shard_map/all_gather | solution.py:103
  208.8 161.0 %all-gather.18.cloned.1.call-start = ((), (), s32[]{:S(2)}) async-start(), calls=%async_computation.15 | async-start | bytes 4239360 | tf_op jit(solution)/shard_map/all_gather | solution.py:135
  209.5 160.3 %copy-start.30 = (f32[1076]{0:T(1024)S(1)}, f32[1076]{0:T(1024)}, u32[]{:S(2)}) copy-start(f32[1076]{0:T(1024)} %param.30) | copy-start | bytes 12916
  209.5 257.2 %reduce-scatter.13.cloned.1.call-start = ((), (), s32[]{:S(2)}) async-start(), calls=%async_computation.16 | async-start | bytes 8478720 | tf_op jit(solution)/shard_map/reduce_scatter | solution.py:151
  369.8 14.9 %copy-start.29 = (bf16[1152,1076]{1,0:T(8,128)(2,1)S(1)}, bf16[1152,1076]{1,0:T(8,128)(2,1)}, u32[]{:S(2)}) copy-start(bf16[1152,1076]{1,0:T(8,128)(2,1)} %all-gather.14.cloned.1.call-done) | copy-start | bytes 7437316
  383.0 1.7 copy-start.33
  391.8 152.7 %reduce-scatter.11.cloned.1.call-start = ((), (), s32[]{:S(2)}) async-start(), calls=%async_computation.14 | async-start | bytes 8478720 | tf_op jit(solution)/shard_map/reduce_scatter | solution.py:132
  404.0 140.5 %copy-start.26 = (f32[1152]{0:T(1024)S(1)}, f32[1152]{0:T(1024)}, u32[]{:S(2)}) copy-start(f32[1152]{0:T(1024)} %param.32) | copy-start | bytes 13828
  404.0 193.4 %all-gather.20.cloned.1.call-start = ((), (), s32[]{:S(2)}) async-start(), calls=%async_computation.17 | async-start | bytes 4239360 | tf_op jit(solution)/shard_map/all_gather | solution.py:157
  549.1 1.2 copy-start.2
  551.3 49.6 %copy-start.5 = (bf16[2,736,4,72]{1,3,2,0:T(8,128)(2,1)S(1)}, bf16[2,736,4,72]{1,3,2,0:T(8,128)(2,1)}, u32[]{:S(2)}) copy-start(bf16[2,736,4,72]{1,3,2,0:T(8,128)(2,1)} %copy-done.4) | copy-start | bytes 2543620
  551.3 227.7 %reduce-scatter.15.cloned.1.call-start = ((), (), s32[]{:S(2)}) async-start(), calls=%async_computation.18 | async-start | bytes 8478720 | tf_op jit(solution)/shard_map/reduce_scatter | solution.py:182
  603.8 3.7 copy-start
  649.6 3.8 copy-start
  692.7 3.8 copy-start.28
  692.7 4.1 copy-start.32
  704.2 139.2 %reduce-scatter.21.cloned.1.call-start = ((), (), s32[]{:S(2)}) async-start(), calls=%async_computation.21 | async-start | bytes 5971968 | tf_op jit(solution)/shard_map/reduce_scatter | solution.py:189
  714.3 0.7 copy-start.31
  714.4 190.7 %reduce-scatter.23.cloned.1.call-start = ((), (), s32[]{:S(2)}) async-start(), calls=%async_computation.22 | async-start | bytes 5971968 | tf_op jit(solution)/shard_map/reduce_scatter | solution.py:190
  726.4 1.4 copy-start.9
  726.4 215.2 %reduce-scatter.19.cloned.1.call-start = ((), (), s32[]{:S(2)}) async-start(), calls=%async_computation.20 | async-start | bytes 1990656 | tf_op jit(solution)/shard_map/reduce_scatter | solution.py:188
  733.2 269.5 %reduce-scatter.17.cloned.1.call-start = ((), (), s32[]{:S(2)}) async-start(), calls=%async_computation.19 | async-start | bytes 5971968 | tf_op jit(solution)/shard_map/reduce_scatter | solution.py:187
  742.8 0.7 copy-start.25
  742.8 36.2 %copy-start.1 = (bf16[2,184,1152]{2,1,0:T(8,128)(2,1)S(1)}, bf16[2,184,1152]{2,1,0:T(8,128)(2,1)}, u32[]{:S(2)}) copy-start(bf16[2,184,1152]{2,1,0:T(8,128)(2,1)} %param.19) | copy-start | bytes 2543620
  742.8 36.2 %copy-start.13 = (f32[1152]{0:T(1024)S(1)}, f32[1152]{0:T(1024)}, u32[]{:S(2)}) copy-start(f32[1152]{0:T(1024)} %param.21) | copy-start | bytes 13828
  742.8 36.2 %copy-start.16 = (f32[2,184]{1,0:T(2,128)S(1)}, f32[2,184]{1,0:T(2,128)}, u32[]{:S(2)}) copy-start(f32[2,184]{1,0:T(2,128)} %copy-done.15) | copy-start | bytes 4420
  742.8 36.2 %copy-start.18 = (f32[2,184]{1,0:T(2,128)S(1)}, f32[2,184]{1,0:T(2,128)}, u32[]{:S(2)}) copy-start(f32[2,184]{1,0:T(2,128)} %copy-done.17) | copy-start | bytes 4420
  742.9 38.5 %copy-start.19 = (f32[1152]{0:T(1024)S(1)}, f32[1152]{0:T(1024)}, u32[]{:S(2)}) copy-start(f32[1152]{0:T(1024)} %get-tuple-element.111) | copy-start | bytes 13828
  742.9 38.5 %copy-start.20 = (f32[1152]{0:T(1024)S(1)}, f32[1152]{0:T(1024)}, u32[]{:S(2)}) copy-start(f32[1152]{0:T(1024)} %get-tuple-element.117) | copy-start | bytes 13828
  742.9 38.5 %copy-start.21 = (f32[1152]{0:T(1024)S(1)}, f32[1152]{0:T(1024)}, u32[]{:S(2)}) copy-start(f32[1152]{0:T(1024)} %get-tuple-element.165) | copy-start | bytes 13828
  742.9 38.5 %copy-start.22 = (f32[1152]{0:T(1024)S(1)}, f32[1152]{0:T(1024)}, u32[]{:S(2)}) copy-start(f32[1152]{0:T(1024)} %get-tuple-element.178) | copy-start | bytes 13828
  742.9 80.6 %copy-start.3 = (f32[2,184,1152]{2,1,0:T(8,128)S(1)}, f32[2,184,1152]{2,1,0:T(8,128)}, u32[]{:S(2)}) copy-start(f32[2,184,1152]{2,1,0:T(8,128)} %copy-done.2) | copy-start | bytes 5087236
Sparse Core Ops, SparseCore 0:
  9.6 40.7 all-gather.9
  52.8 46.1 all-gather.7
  129.8 74.7 reduce-scatter.8
  206.1 33.9 all-gather.13
  242.4 44.9 all-gather.11
  288.9 33.9 all-gather.15
  324.8 45.0 all-gather.17
  391.9 74.7 reduce-scatter.12
  469.7 74.7 reduce-scatter.10
  551.5 45.8 all-gather.19
  704.3 74.7 reduce-scatter.14
  781.8 61.4 reduce-scatter.20
  846.2 58.8 reduce-scatter.22
  907.9 33.7 reduce-scatter.18
  944.4 58.2 reduce-scatter.16
where the time goes:
time: 1010 us
  waiting for transfers between devices  655 us (65%)
  matrix products  200 us (20%)
  blocking collectives  93.9 us (9%)
  other arithmetic  34.3 us (3%)
  between operations  14.5 us (1%)
    reduce_scatter x1, waiting for transfers between devices, shards(): lax.psum_scatter(mlp_part, 'tensor', scatter_dimension=1, tiled=True)  75 us
    reduce_scatter x1, waiting for transfers between devices, shards(): lax.psum_scatter(attn_part, 'tensor', scatter_dimension=1, tiled=True)  74.2 us
    reduce_scatter x1, waiting for transfers between devices, shards(): lax.psum_scatter(normed_two_part, 'tensor', scatter_dimension=1, tiled=True)  62.7 us
    reduce_scatter x1, waiting for transfers between devices, shards(): lax.psum_scatter(grad_down_w, 'dp', scatter_dimension=1, tiled=True)  61.8 us
    reduce_scatter x1, waiting for transfers between devices, shards(): lax.psum_scatter(grad_qkv_w, 'dp', scatter_dimension=0, tiled=True)  61 us
    all_gather x1, waiting for transfers between devices, shards(): gathered_one = lax.all_gather(normed_one, 'tensor', axis=1, tiled=True)  48.7 us
    all_gather x1, waiting for transfers between devices, shards(): gathered_two = lax.all_gather(normed_two, 'tensor', axis=1, tiled=True)  47.3 us
    all_gather x1, waiting for transfers between devices, shards(): grad_full = lax.all_gather(grad_out, 'tensor', axis=1, tiled=True)  46.9 us
  transfers between devices with their start and end apart: 15, of which 15 were waited for; matrix products, arithmetic and copies ran while one was open for 8% of the time, Pallas kernels for 0%

commit v1 on v0

v1 whole, which is shorter than its diff:
```python
import functools
import math

import jax
import jax.numpy as jnp
from jax import lax
from jax.experimental import pallas as pl
from jax.experimental.pallas import tpu as pltpu
from jax.sharding import PartitionSpec as P

HD = 72
CHUNK = 768
F32 = jnp.float32
BF16 = jnp.bfloat16
LOG2E = math.log2(math.e)
NN = (((1,), (0,)), ((), ()))
NT = (((1,), (1,)), ((), ()))
MESH = pl.DeviceIdType.MESH
ANY = pl.BlockSpec(memory_space=pl.ANY)
VMEM = pl.BlockSpec(memory_space=pltpu.VMEM)
SMEM = pl.BlockSpec(memory_space=pltpu.SMEM)


layer_eps = 1e-06
gelu_root = math.sqrt(2.0 / math.pi)
gelu_cubic = 0.044715


def norm_stats(rows):
    center = rows - jnp.mean(rows, axis=-1, keepdims=True)
    inv_std = lax.rsqrt(jnp.mean(center * center, axis=-1, keepdims=True) + layer_eps)
    return (center * inv_std, inv_std)


def norm_forward(rows, gain, shift):
    unit, _ = norm_stats(rows)
    return (unit * gain + shift).astype(BF16)


def norm_backward(grad_normed, unit, inv_std, gain):
    scaled = grad_normed * gain
    return inv_std * (
        scaled
        - jnp.mean(scaled, axis=-1, keepdims=True)
        - unit * jnp.mean(scaled * unit, axis=-1, keepdims=True)
    )


def gelu_both(pre):
    tangent = jnp.tanh(gelu_root * (pre + gelu_cubic * pre * pre * pre))
    value = 0.5 * pre * (1.0 + tangent)
    slope = 0.5 * (1.0 + tangent) + 0.5 * pre * (1.0 - tangent * tangent) * gelu_root * (
        1.0 + 3.0 * gelu_cubic * pre * pre
    )
    return (value, slope)


def dot(a, b, dims=NN):
    return lax.dot_general(a, b, dims, preferred_element_type=F32)


def soft_columns(keys_in, queries, row_ok, factor):
    raw = jnp.where(row_ok, dot(keys_in, queries, NT), -1e30)
    top = jnp.max(raw, axis=0, keepdims=True)
    grown = jnp.exp2((raw - top) * factor)
    total = jnp.sum(grown, axis=0, keepdims=True)
    return grown * (1.0 / total)


def attend_forward_body(seq, heads, lens_ref, proj_ref, mixed_ref, qh, kh, vh, oh):
    width = heads * HD
    padded = qh.shape[1]
    for h in range(heads):
        qh[h, :seq] = proj_ref[0, :, h * HD : (h + 1) * HD]
        qh[h, seq:] = jnp.zeros((padded - seq, HD), BF16)
        kh[h] = proj_ref[0, :, width + h * HD : width + (h + 1) * HD]
        vh[h] = proj_ref[0, :, 2 * width + h * HD : 2 * width + (h + 1) * HD].T
    length = lens_ref[pl.program_id(0)]
    factor = HD**-0.5 * LOG2E

    def head(h, _):
        def chunk(c, _):
            row_ok = lax.broadcasted_iota(jnp.int32, (seq, CHUNK), 0) < length
            at = pl.ds(pl.multiple_of(c * CHUNK, CHUNK), CHUNK)
            probs = soft_columns(kh[h], qh[h, at], row_ok, factor)
            oh[h, at] = dot(vh[h], probs.astype(BF16)).T.astype(BF16)
            return 0

        return lax.fori_loop(0, padded // CHUNK, chunk, 0)

    lax.fori_loop(0, heads, head, 0)
    for h in range(heads):
        mixed_ref[0, :, h * HD : (h + 1) * HD] = oh[h, :seq]


def attend_forward(lens, proj):
    images, seq, triple = proj.shape
    heads = triple // (3 * HD)
    padded = -(-seq // CHUNK) * CHUNK
    return pl.pallas_call(
        functools.partial(attend_forward_body, seq, heads),
        out_shape=jax.ShapeDtypeStruct((images, seq, heads * HD), BF16),
        grid=(images,),
        in_specs=[SMEM, pl.BlockSpec((1, seq, triple), lambda i: (i, 0, 0))],
        out_specs=pl.BlockSpec((1, seq, heads * HD), lambda i: (i, 0, 0)),
        scratch_shapes=[
            pltpu.VMEM((heads, padded, HD), BF16),
            pltpu.VMEM((heads, seq, HD), BF16),
            pltpu.VMEM((heads, HD, seq), BF16),
            pltpu.VMEM((heads, padded, HD), BF16),
        ],
        name="attend_forward",
    )(lens, proj)


def attend_backward_body(
    seq, heads, lens_ref, proj_ref, gmix_ref, gproj_ref, gbias_ref, qh, kh, kt, vh, gh, gq, gk, gv
):
    width = heads * HD
    padded = qh.shape[1]
    for h in range(heads):
        qh[h, :seq] = proj_ref[0, :, h * HD : (h + 1) * HD]
        qh[h, seq:] = jnp.zeros((padded - seq, HD), BF16)
        gh[h, :seq] = gmix_ref[0, :, h * HD : (h + 1) * HD]
        gh[h, seq:] = jnp.zeros((padded - seq, HD), BF16)
        keys_in = proj_ref[0, :, width + h * HD : width + (h + 1) * HD]
        kh[h] = keys_in
        kt[h] = keys_in.T
        vh[h] = proj_ref[0, :, 2 * width + h * HD : 2 * width + (h + 1) * HD]
    length = lens_ref[pl.program_id(0)]
    scale = HD**-0.5
    factor = scale * LOG2E

    def head(h, _):
        gk[h] = jnp.zeros((seq, HD), F32)
        gv[h] = jnp.zeros((seq, HD), F32)

        def chunk(c, _):
            row_ok = lax.broadcasted_iota(jnp.int32, (seq, CHUNK), 0) < length
            at = pl.ds(pl.multiple_of(c * CHUNK, CHUNK), CHUNK)
            queries = qh[h, at]
            grads = gh[h, at]
            probs = soft_columns(kh[h], queries, row_ok, factor)
            grad_probs = dot(vh[h], grads, NT)
            gv[h] += dot(probs.astype(BF16), grads)
            delta = jnp.sum(probs * grad_probs, axis=0, keepdims=True)
            grad_scores = (probs * (grad_probs - delta) * scale).astype(BF16)
            gk[h] += dot(grad_scores, queries)
            gq[h, at] = dot(kt[h], grad_scores).T
            return 0

        return lax.fori_loop(0, padded // CHUNK, chunk, 0)

    lax.fori_loop(0, heads, head, 0)
    for h in range(heads):
        for c, held in enumerate((gq, gk, gv)):
            value = held[h, :seq]
            at = slice(c * width + h * HD, c * width + (h + 1) * HD)
            gproj_ref[0, :, at] = value.astype(BF16)
            gbias_ref[0, :, at] = jnp.sum(value, axis=0, keepdims=True)


def attend_backward(lens, proj, gmix):
    images, seq, triple = proj.shape
    heads = triple // (3 * HD)
    padded = -(-seq // CHUNK) * CHUNK
    return pl.pallas_call(
        functools.partial(attend_backward_body, seq, heads),
        out_shape=(
            jax.ShapeDtypeStruct((images, seq, triple), BF16),
            jax.ShapeDtypeStruct((images, 1, triple), F32),
        ),
        grid=(images,),
        in_specs=[
            SMEM,
            pl.BlockSpec((1, seq, triple), lambda i: (i, 0, 0)),
            pl.BlockSpec((1, seq, heads * HD), lambda i: (i, 0, 0)),
        ],
        out_specs=(
            pl.BlockSpec((1, seq, triple), lambda i: (i, 0, 0)),
            pl.BlockSpec((1, 1, triple), lambda i: (i, 0, 0)),
        ),
        scratch_shapes=[
            pltpu.VMEM((heads, padded, HD), BF16),
            pltpu.VMEM((heads, seq, HD), BF16),
            pltpu.VMEM((heads, HD, seq), BF16),
            pltpu.VMEM((heads, seq, HD), BF16),
            pltpu.VMEM((heads, padded, HD), BF16),
            pltpu.VMEM((heads, padded, HD), F32),
            pltpu.VMEM((heads, seq, HD), F32),
            pltpu.VMEM((heads, seq, HD), F32),
        ],
        name="attend_backward",
    )(lens, proj, gmix)


def plane():
    me = lax.axis_index("tensor")
    side = me + 1 - 2 * lax.rem(me, 2)
    over = lax.rem(me + 2, 4)
    return (me, side, over, lax.rem(side + 2, 4))


def greet(peers):
    barrier = pltpu.get_barrier_semaphore()
    for peer in peers:
        pl.semaphore_signal(barrier, inc=1, device_id={"tensor": peer}, device_id_type=MESH)
    pl.semaphore_wait(barrier, len(peers))


def remote(src, dst, send, recv, peer):
    return pltpu.make_async_remote_copy(
        src_ref=src,
        dst_ref=dst,
        send_sem=send,
        recv_sem=recv,
        device_id={"tensor": peer},
        device_id_type=MESH,
    )


def halves_of(rows):
    first = -(-rows // 32) * 16
    return (pl.ds(0, first), pl.ds(first, rows - first))


class Gather:
    def __init__(self, all_ref, send, recv):
        self.me, self.side, self.over, _ = plane()
        self.all_ref, self.send, self.recv = all_ref, send, recv
        self.low, self.high = halves_of(all_ref.shape[1])
        self.done = []

    def copy(self, k, block, rows, peer):
        part = self.all_ref.at[block, rows]
        made = remote(part, part, self.send.at[k], self.recv.at[k], peer)
        made.start()
        self.done.append(made)
        return made

    def start(self):
        self.first = self.copy(0, self.me, self.low, self.side)
        self.second = self.copy(1, self.me, self.high, self.over)
        self.copy(2, self.me, self.high, self.side)
        self.copy(3, self.me, self.low, self.over)

    def forward(self):
        self.first.wait_recv()
        self.copy(4, self.side, self.low, self.over)
        self.second.wait_recv()
        self.copy(5, self.over, self.high, self.side)

    def finish(self):
        for made in self.done:
            if made is not self.first and made is not self.second:
                made.wait_recv()
            made.wait_send()


class Scatter:
    def __init__(self, part_ref, near_ref, far_ref, pass_ref, send, recv):
        self.me, self.side, self.over, self.cross = plane()
        self.part_ref, self.near_ref, self.far_ref, self.pass_ref = part_ref, near_ref, far_ref, pass_ref
        self.send, self.recv = send, recv
        self.halves = halves_of(part_ref.shape[1])
        self.done = []

    def copy(self, k, src, dst, peer):
        made = remote(src, dst, self.send.at[k], self.recv.at[k], peer)
        made.start()
        self.done.append(made)
        return made

    def near(self, half, slot):
        return self.near_ref.at[slot, self.halves[half]]

    def start(self):
        low, high = self.halves
        part = self.part_ref
        self.first = self.copy(0, part.at[self.cross, low], self.near(0, 1), self.side)
        self.second = self.copy(1, part.at[self.cross, high], self.near(1, 1), self.over)
        self.third = self.copy(2, part.at[self.side, low], self.near(0, 0), self.side)
        self.fourth = self.copy(3, part.at[self.over, high], self.near(1, 0), self.over)

    def forward(self):
        low, high = self.halves
        self.first.wait_recv()
        self.pass_ref[low] = (
            self.part_ref[self.over, low].astype(F32) + self.near_ref[1, low].astype(F32)
        ).astype(BF16)
        self.fifth = self.copy(4, self.pass_ref.at[low], self.far_ref.at[low], self.over)
        self.second.wait_recv()
        self.pass_ref[high] = (
            self.part_ref[self.side, high].astype(F32) + self.near_ref[1, high].astype(F32)
        ).astype(BF16)
        self.sixth = self.copy(5, self.pass_ref.at[high], self.far_ref.at[high], self.side)

    def arrive(self):
        for made in (self.third, self.fourth, self.fifth, self.sixth):
            made.wait_recv()

    def total(self, rows):
        return (
            self.part_ref[self.me, rows].astype(F32)
            + self.near_ref[0, rows].astype(F32)
            + self.far_ref[rows].astype(F32)
        )

    def finish(self):
        for made in self.done:
            made.wait_send()


STEPS = 6


def sems(*shape):
    return [pltpu.SemaphoreType.DMA(shape), pltpu.SemaphoreType.DMA(shape)]


def scatter_scratch(images, rows, width):
    return [
        pltpu.VMEM((images, 2, rows, width), BF16),
        pltpu.VMEM((images, rows, width), BF16),
        pltpu.VMEM((images, rows, width), BF16),
    ]


def params(cid):
    return pltpu.CompilerParams(collective_id=cid, has_side_effects=True, vmem_limit_bytes=60 << 20)


def open_body(x_ref, gain_ref, shift_ref, grad_ref, normed_ref, gfull_ref, send, recv):
    images, rows, _ = x_ref.shape
    me, side, over, _ = plane()
    greet((side, over))
    gathers = []
    for i in range(images):
        normed_ref[i, me] = norm_forward(x_ref[i].astype(F32), gain_ref[...], shift_ref[...])
        step = Gather(normed_ref.at[i], send.at[0, i], recv.at[0, i])
        step.start()
        gathers.append(step)
    for i in range(images):
        gfull_ref[i, me] = grad_ref[i]
        gathers[i].forward()
    more = []
    for i in range(images):
        step = Gather(gfull_ref.at[i], send.at[1, i], recv.at[1, i])
        step.start()
        more.append(step)
    for step in more:
        step.forward()
    for step in gathers + more:
        step.finish()


def open_plane(block_input, gain, shift, grad_out):
    images, rows, width = block_input.shape
    full = jax.ShapeDtypeStruct((images, 4, rows, width), BF16)
    return pl.pallas_call(
        open_body,
        out_shape=(full, full),
        in_specs=[VMEM] * 4,
        out_specs=(VMEM, VMEM),
        scratch_shapes=sems(2, images, STEPS),
        compiler_params=params(0),
        name="open_plane",
    )(block_input, gain, shift, grad_out)


def middle_body(
    part_ref, x_ref, bias_ref, gain_ref, shift_ref, hidden_ref, normed_ref, near, far, passing, ssend, srecv, gsend, grecv
):
    images, rows, _ = x_ref.shape
    me, side, over, _ = plane()
    greet((side, over))
    sums = []
    for i in range(images):
        step = Scatter(part_ref.at[i], near.at[i], far.at[i], passing.at[i], ssend.at[i], srecv.at[i])
        step.start()
        sums.append(step)
    for step in sums:
        step.forward()
    gathers = []
    for i in range(images):
        sums[i].arrive()
        hidden = x_ref[i].astype(F32) + sums[i].total(pl.ds(0, rows)) + bias_ref[...]
        hidden_ref[i] = hidden
        normed_ref[i, me] = norm_forward(hidden, gain_ref[...], shift_ref[...])
        step = Gather(normed_ref.at[i], gsend.at[i], grecv.at[i])
        step.start()
        gathers.append(step)
    for step in gathers:
        step.forward()
    for step in sums + gathers:
        step.finish()


def middle_plane(part, block_input, bias, gain, shift):
    images, rows, width = block_input.shape
    return pl.pallas_call(
        middle_body,
        out_shape=(
            jax.ShapeDtypeStruct((images, rows, width), F32),
            jax.ShapeDtypeStruct((images, 4, rows, width), BF16),
        ),
        in_specs=[VMEM] * 5,
        out_specs=(VMEM, VMEM),
        scratch_shapes=scatter_scratch(images, rows, width) + sems(images, STEPS) + sems(images, STEPS),
        compiler_params=params(1),
        name="middle_plane",
    )(part, block_input, bias, gain, shift)


def turn_body(
    gpart_ref, mpart_ref, hidden_ref, grad_ref, gain_ref, dbias_ref,
    out_ref, ghid_ref, glow_ref, sums_ref,
    near, far, passing, near2, far2, passing2, ssend, srecv, msend, mrecv, gsend, grecv,
):
    images, rows, _ = hidden_ref.shape
    me, side, over, _ = plane()
    greet((side, over))
    sums, outs = [], []
    for i in range(images):
        step = Scatter(gpart_ref.at[i], near.at[i], far.at[i], passing.at[i], ssend.at[i], srecv.at[i])
        step.start()
        sums.append(step)
    for step in sums:
        step.forward()
    for i in range(images):
        step = Scatter(mpart_ref.at[i], near2.at[i], far2.at[i], passing2.at[i], msend.at[i], mrecv.at[i])
        outs.append(step)
    outs[0].start()
    gathers = []
    totals = [0.0, 0.0, 0.0, 0.0]
    for i in range(images):
        sums[i].arrive()
        grad_normed = sums[i].total(pl.ds(0, rows))
        unit, inv_std = norm_stats(hidden_ref[i])
        upper = grad_ref[i].astype(F32)
        grad_hidden = upper + norm_backward(grad_normed, unit, inv_std, gain_ref[...])
        ghid_ref[i] = grad_hidden
        glow_ref[i, me] = grad_hidden.astype(BF16)
        step = Gather(glow_ref.at[i], gsend.at[i], grecv.at[i])
        step.start()
        gathers.append(step)
        for k, term in enumerate((grad_normed * unit, grad_normed, grad_hidden, upper)):
            totals[k] = totals[k] + jnp.sum(term, axis=0, keepdims=True)
    for k in range(4):
        sums_ref[k : k + 1] = totals[k]
    outs[0].forward()
    for step in gathers:
        step.forward()
    for step in outs[1:]:
        step.start()
    for step in outs[1:]:
        step.forward()
    for i in range(images):
        outs[i].arrive()
        out_ref[i] = (hidden_ref[i] + outs[i].total(pl.ds(0, rows)) + dbias_ref[...]).astype(BF16)
    for step in sums + outs + gathers:
        step.finish()


def turn_plane(gpart, mpart, hidden, grad_out, gain, dbias):
    images, rows, width = hidden.shape
    return pl.pallas_call(
        turn_body,
        out_shape=(
            jax.ShapeDtypeStruct((images, rows, width), BF16),
            jax.ShapeDtypeStruct((images, rows, width), F32),
            jax.ShapeDtypeStruct((images, 4, rows, width), BF16),
            jax.ShapeDtypeStruct((4, width), F32),
        ),
        in_specs=[VMEM] * 6,
        out_specs=(VMEM,) * 4,
        scratch_shapes=scatter_scratch(images, rows, width) * 2 + sems(images, STEPS) * 3,
        compiler_params=params(2),
        name="turn_plane",
    )(gpart, mpart, hidden, grad_out, gain, dbias)


def close_body(
    part_ref, x_ref, ghid_ref, gain_ref, out_ref, sums_ref, near, far, passing, ssend, srecv
):
    images, rows, _ = x_ref.shape
    me, side, over, _ = plane()
    greet((side, over))
    sums = []
    for i in range(images):
        step = Scatter(part_ref.at[i], near.at[i], far.at[i], passing.at[i], ssend.at[i], srecv.at[i])
        step.start()
        sums.append(step)
    for step in sums:
        step.forward()
    totals = [0.0, 0.0]
    for i in range(images):
        sums[i].arrive()
        grad_normed = sums[i].total(pl.ds(0, rows))
        unit, inv_std = norm_stats(x_ref[i].astype(F32))
        out_ref[i] = ghid_ref[i] + norm_backward(grad_normed, unit, inv_std, gain_ref[...])
        for k, term in enumerate((grad_normed * unit, grad_normed)):
            totals[k] = totals[k] + jnp.sum(term, axis=0, keepdims=True)
    for k in range(2):
        sums_ref[k : k + 1] = totals[k]
    for step in sums:
        step.finish()


def close_plane(part, block_input, ghid, gain):
    images, rows, width = block_input.shape
    return pl.pallas_call(
        close_body,
        out_shape=(
            jax.ShapeDtypeStruct((images, rows, width), F32),
            jax.ShapeDtypeStruct((2, width), F32),
        ),
        in_specs=[VMEM] * 4,
        out_specs=(VMEM, VMEM),
        scratch_shapes=scatter_scratch(images, rows, width) + sems(images, STEPS),
        compiler_params=params(3),
        name="close_plane",
    )(part, block_input, ghid, gain)


def small_body(groups, both_ref, own_ref, both_out, own_out, both_in, own_in, side_in, over_in, held, send, recv, psend, precv):
    row = lax.axis_index("dp")
    me, side, over, _ = plane()
    barrier = pltpu.get_barrier_semaphore()
    for k in range(1, groups):
        pl.semaphore_signal(
            barrier, inc=1, device_id={"dp": lax.rem(row + k, groups)}, device_id_type=MESH
        )
    for peer in (side, over):
        pl.semaphore_signal(barrier, inc=1, device_id={"tensor": peer}, device_id_type=MESH)
    pl.semaphore_wait(barrier, groups + 1)
    copies = []
    for k in range(1, groups):
        for j, (src, dst) in enumerate(((both_ref, both_in), (own_ref, own_in))):
            made = pltpu.make_async_remote_copy(
                src_ref=src,
                dst_ref=dst.at[row],
                send_sem=send.at[j, k],
                recv_sem=recv.at[j, k],
                device_id={"dp": lax.rem(row + k, groups)},
                device_id_type=MESH,
            )
            made.start()
            copies.append(made)
    both_in[row] = both_ref[...]
    own_in[row] = own_ref[...]
    for made in copies:
        made.wait()
    held[0] = jnp.sum(both_in[...], axis=0)
    own_out[...] = jnp.sum(own_in[...], axis=0)
    first = remote(held.at[0], side_in, psend.at[0], precv.at[0], side)
    first.start()
    first.wait()
    held[1] = held[0] + side_in[...]
    second = remote(held.at[1], over_in, psend.at[1], precv.at[1], over)
    second.start()
    second.wait()
    both_out[...] = held[1] + over_in[...]


def small_sums(groups, both, own):
    return pl.pallas_call(
        functools.partial(small_body, groups),
        out_shape=(
            jax.ShapeDtypeStruct(both.shape, F32),
            jax.ShapeDtypeStruct(own.shape, F32),
        ),
        in_specs=[VMEM] * 2,
        out_specs=(VMEM, VMEM),
        scratch_shapes=[
            pltpu.VMEM((groups,) + both.shape, F32),
            pltpu.VMEM((groups,) + own.shape, F32),
            pltpu.VMEM(both.shape, F32),
            pltpu.VMEM(both.shape, F32),
            pltpu.VMEM((2,) + both.shape, F32),
        ]
        + sems(2, groups)
        + sems(2),
        compiler_params=params(4),
        name="small_sums",
    )(both, own)


def gather_rows(rows):
    return lax.all_gather(rows, "tensor", axis=1, tiled=True)


def scatter_rows(part):
    return lax.psum_scatter(part, "tensor", scatter_dimension=1, tiled=True).astype(F32)


def shards(
    groups,
    ranks,
    block_input,
    key_mask,
    attn_norm_gain,
    attn_norm_bias,
    qkv_weight,
    qv_bias,
    out_weight,
    out_bias,
    mlp_norm_gain,
    mlp_norm_bias,
    hidden_weight,
    hidden_bias,
    down_weight,
    down_bias,
    grad_out,
):
    flat = ranks == 4
    images, rows, model = block_input.shape
    seq = key_mask.shape[1]
    width = qkv_weight.shape[2]
    units = hidden_weight.shape[1]
    row = lambda v: v.reshape(1, -1)
    whole = lambda v: v.reshape(images, seq, model)
    split = lambda v: v.reshape(images, ranks, rows, model)

    def weight(shard):
        return lax.all_gather(shard, "dp", axis=0, tiled=True)

    def owned(grad):
        return lax.psum_scatter(grad.astype(BF16), "dp", scatter_dimension=0, tiled=True).astype(F32)

    qkv_all = weight(qkv_weight.reshape(-1, 3 * width))
    out_all = weight(out_weight.T)
    hidden_all = weight(hidden_weight)
    down_all = weight(down_weight.T)

    lens = jnp.sum(key_mask, axis=1)
    if flat:
        normed_one, grad_full = open_plane(
            block_input, row(attn_norm_gain), row(attn_norm_bias), grad_out
        )
        normed_one, grad_full = whole(normed_one), whole(grad_full)
    else:
        in_float = block_input.astype(F32)
        normed_one = gather_rows(norm_forward(in_float, attn_norm_gain, attn_norm_bias))
        grad_full = gather_rows(grad_out)

    shift = jnp.concatenate([qv_bias[0], jnp.zeros_like(qv_bias[0]), qv_bias[1]])
    proj = jnp.einsum("isd,df->isf", normed_one, qkv_all, preferred_element_type=F32) + shift
    proj = proj.astype(BF16)
    mixed = attend_forward(lens, proj)
    attn_part = jnp.einsum("isf,df->isd", mixed, out_all, preferred_element_type=F32).astype(BF16)
    if flat:
        hidden_res, normed_two = middle_plane(
            split(attn_part), block_input, row(out_bias), row(mlp_norm_gain), row(mlp_norm_bias)
        )
        normed_two = whole(normed_two)
    else:
        hidden_res = in_float + scatter_rows(attn_part) + out_bias
        normed_two = gather_rows(norm_forward(hidden_res, mlp_norm_gain, mlp_norm_bias))

    pre_act = jnp.einsum("isd,df->isf", normed_two, hidden_all, preferred_element_type=F32) + hidden_bias
    value, slope = gelu_both(pre_act)
    activated = value.astype(BF16)
    grad_act = jnp.einsum("isd,df->isf", grad_full, down_all, preferred_element_type=F32)
    grad_pre = grad_act * slope
    grad_hidden_b = jnp.sum(grad_pre, axis=(0, 1))
    grad_pre_low = grad_pre.astype(BF16)
    gpart = jnp.einsum("isf,df->isd", grad_pre_low, hidden_all, preferred_element_type=F32).astype(BF16)
    mpart = jnp.einsum("isf,df->isd", activated, down_all, preferred_element_type=F32).astype(BF16)
    if flat:
        block_output, grad_hidden, hidden_full, mlp_sums = turn_plane(
            split(gpart), split(mpart), hidden_res, grad_out, row(mlp_norm_gain), row(down_bias)
        )
        hidden_full = whole(hidden_full)
    else:
        block_output = (hidden_res + scatter_rows(mpart) + down_bias).astype(BF16)
        grad_float = grad_out.astype(F32)
        grad_normed = scatter_rows(gpart)
        unit, inv_std = norm_stats(hidden_res)
        grad_hidden = grad_float + norm_backward(grad_normed, unit, inv_std, mlp_norm_gain)
        hidden_full = gather_rows(grad_hidden.astype(BF16))
        mlp_sums = jnp.stack(
            [jnp.sum(v, axis=(0, 1)) for v in (grad_normed * unit, grad_normed, grad_hidden, grad_float)]
        )
    grad_hidden_w = owned(jnp.einsum("isd,isf->df", normed_two, grad_pre_low, preferred_element_type=F32))
    grad_down_w = owned(jnp.einsum("isd,isf->df", grad_full, activated, preferred_element_type=F32))

    grad_mixed = jnp.einsum("isd,df->isf", hidden_full, out_all, preferred_element_type=F32).astype(BF16)
    grad_proj, proj_sums = attend_backward(lens, proj, grad_mixed)
    npart = jnp.einsum("isf,df->isd", grad_proj, qkv_all, preferred_element_type=F32).astype(BF16)
    grad_out_w = owned(jnp.einsum("isd,isf->df", hidden_full, mixed, preferred_element_type=F32))
    grad_qkv_w = owned(jnp.einsum("isd,isf->df", normed_one, grad_proj, preferred_element_type=F32))
    if flat:
        grad_input, attn_sums = close_plane(split(npart), block_input, grad_hidden, row(attn_norm_gain))
    else:
        grad_normed = scatter_rows(npart)
        unit, inv_std = norm_stats(in_float)
        grad_input = grad_hidden + norm_backward(grad_normed, unit, inv_std, attn_norm_gain)
        attn_sums = jnp.stack([jnp.sum(v, axis=(0, 1)) for v in (grad_normed * unit, grad_normed)])

    both = jnp.concatenate([mlp_sums, attn_sums])
    proj_sums = jnp.sum(proj_sums, axis=(0, 1))
    own = jnp.concatenate([proj_sums[:width], proj_sums[2 * width :], grad_hidden_b])
    if flat:
        pad = -own.shape[0] % 1024
        both, own = small_sums(
            groups, jnp.pad(both, ((0, 2), (0, 0))), jnp.pad(own, (0, pad)).reshape(8, -1)
        )
        own = own.reshape(-1)
    else:
        both = lax.psum(both, ("dp", "tensor"))
        own = lax.psum(own, "dp")
    return (
        block_output,
        grad_input,
        both[4],
        both[5],
        grad_qkv_w.reshape(-1, 3, width),
        own[: 2 * width].reshape(2, width),
        grad_out_w.T,
        both[2],
        both[0],
        both[1],
        grad_hidden_w,
        own[2 * width : 2 * width + units],
        grad_down_w.T,
        both[3],
    )


def solution(mesh):
    return jax.shard_map(
        functools.partial(shards, mesh.shape["dp"], mesh.shape["tensor"]),
        mesh=mesh,
        in_specs=(
            P("dp", "tensor", None),
            P("dp", None),
            P(),
            P(),
            P("dp", None, "tensor"),
            P(None, "tensor"),
            P("tensor", "dp"),
            P(),
            P(),
            P(),
            P("dp", "tensor"),
            P("tensor"),
            P("tensor", "dp"),
            P(),
            P("dp", "tensor", None),
        ),
        out_specs=(
            P("dp", "tensor", None),
            P("dp", "tensor", None),
            P(),
            P(),
            P("dp", None, "tensor"),
            P(None, "tensor"),
            P("tensor", "dp"),
            P(),
            P(),
            P(),
            P("dp", "tensor"),
            P("tensor"),
            P("tensor", "dp"),
            P(),
        ),
        check_vma=False,
    )
```

time: 1010 us -> 508 us (0.50)
  waiting for transfers between devices: 655 us -> 12 us
  Pallas kernels: 0 us -> 318 us
  matrix products: 200 us -> 95.9 us
  blocking collectives: 93.9 us -> 22 us
  other arithmetic: 34.3 us -> 8.13 us
  local copies, waits for them, and re-layouts: 9.44 us -> 20.7 us
  starting transfers between devices: 1.94 us -> 12.1 us
    reduce_scatter x8 -> x4, waiting for transfers between devices: 395 us -> 10.6 us  [owned(): lax.psum_scatter(grad.astype(BF16), 'dp', scatter_dimension=0, tiled=True)]
    pallas_call x0 -> x7, Pallas kernels: none -> 318 us  [the longest x1 91.5 us: turn_plane(): pl.pallas_call(turn_body, out_shape=(jax.ShapeDtypeStruct((images, rows,...]
    all_gather x7 -> x3, waiting for transfers between devices: 258 us -> 0.02 us  [weight(): return lax.all_gather(shard, 'dp', axis=0, tiled=True)]
    dot_general x25 -> x11, matrix products: 193 us -> 89 us  [the longest x1 11.6 us: shards(): jnp.einsum('isf,df->isd', activated, down_all, preferred_element_type=F32)]
    psum x2 -> x0, blocking collectives: 70.5 us -> none  [the longest x1 42.2 us: shards(): lax.psum((grad_attn_gain, grad_attn_shift, grad_out_b, grad_mlp_gain, gra...]
    reduce_sum x10 -> x2, other arithmetic: 23 us -> 1.34 us  [the longest x1 1.32 us: shards(): lens = jnp.sum(key_mask, axis=1)]
    reshape x0 -> x10, local copies, waits for them, and re-layouts: none -> 11.6 us  [the longest x6 7.76 us: shards(): row = lambda v: v.reshape(1, -1)]
    reduce_scatter x8 -> x4, starting transfers between devices: 1.66 us -> 12 us  [owned(): lax.psum_scatter(grad.astype(BF16), 'dp', scatter_dimension=0, tiled=True)]
  transfers between devices with their start and end apart: 15 -> 7, of which waited for: 15 -> 1; matrix products, arithmetic and copies ran while one was open for 8% -> 17% of each run, Pallas kernels for 0% -> 45%
where the time goes in v1:
time: 508 us; the launch traced here: 503 us
  Pallas kernels  318 us (63%)
  matrix products  95.9 us (19%)
  blocking collectives  22 us (4%)
  local copies, waits for them, and re-layouts  20.7 us (4%)
  between operations  14.6 us (3%)
  starting transfers between devices  12.1 us (2%)
  waiting for transfers between devices  12 us (2%)
  other arithmetic  8.13 us (2%)
    pallas_call x1, Pallas kernels, turn_plane(): pl.pallas_call(turn_body, out_shape=(jax.ShapeDtypeStruct((images, rows,...  91.5 us
    pallas_call x1, Pallas kernels, open_plane(): pl.pallas_call(open_body, out_shape=(full, full), in_specs=[VMEM] * 4, ou...  65.3 us
    pallas_call x1, Pallas kernels, middle_plane(): pl.pallas_call(middle_body, out_shape=(jax.ShapeDtypeStruct((images, rows...  62.4 us
    pallas_call x1, Pallas kernels, close_plane(): pl.pallas_call(close_body, out_shape=(jax.ShapeDtypeStruct((images, rows,...  34.1 us
    pallas_call x1, Pallas kernels, attend_backward(): pl.pallas_call(functools.partial(attend_backward_body, seq, heads), out_s...  28.8 us
    all_gather x1, blocking collectives, weight(): return lax.all_gather(shard, 'dp', axis=0, tiled=True)  22 us
    pallas_call x1, Pallas kernels, small_sums(): pl.pallas_call(functools.partial(small_body, groups), out_shape=(jax.Shap...  19.7 us
    pallas_call x1, Pallas kernels, attend_forward(): pl.pallas_call(functools.partial(attend_forward_body, seq, heads), out_sh...  16.2 us
  transfers between devices with their start and end apart: 7, of which 1 were waited for; matrix products, arithmetic and copies ran while one was open for 17% of the time, Pallas kernels for 45%

profile of v1, /device:TPU:0, one launch (start us, length us, event | category | flops | bytes accessed | tf_op | source)
XLA Modules:
  0.0 503.5 jit_solution(4102349105358230284)
XLA Ops:
  7.2 0.0 all-gather.6.cloned.1.call-start
  7.2 1.2 copy.39
  8.4 1.0 reshape.96
  9.4 0.0 all-gather.6.cloned.1.call-update
  9.4 0.0 all-gather.8.cloned.1.call-start
  9.5 0.7 all-gather.8.cloned.1.call-update
  10.2 0.0 all-gather.4.cloned.1.call-start
  10.2 0.7 all-gather.4.cloned.1.call-update
  10.9 0.0 reduce-scatter.7.cloned.1.call-start
  10.9 1.3 reshape.92.gain_ref
  12.2 1.3 reshape.99.gain_ref
  13.5 1.3 reshape.93.shift_ref
  14.8 1.3 reshape.98.bias_ref
  16.1 1.3 reshape.100.shift_ref
  17.4 1.3 reshape.104.dbias_ref
  18.7 1.3 reduce_sum.27.lens_ref
  20.0 65.3 %open_plane.1 = (bf16[2,4,184,1152]{3,2,1,0:T(8,128)(2,1)}, bf16[2,4,184,1152]{3,2,1,0:T(8,128)(2,1)}) custom-call(bf16[2,184,1152]{2,1,0:T(8,128)(2,1)} %x_ref.5, f32[1,1152]{1,0:T(1,128)} %reshape.92.gain_ref, f32[1,1152]{1,0:T(1,128)} %reshape.93.shift_ref, bf16[2,184,1152]{2,1,0:T(8,128)(2,1)} %grad_ref.3), custom_call_target="tpu_custom_call" | custom-call | tf_op jit(solution)/shard_map/open_plane/pallas_call | solution.py:360
  85.4 0.1 pad_maximum_fusion
  85.5 22.0 %all_gather.14 = bf16[1152,288]{1,0:T(8,128)(2,1)S(1)} all-gather(bf16[144,288]{1,0:T(8,128)(2,1)S(1)} %bitcast.71), channel_id=1, replica_groups=mesh['dp'=8,'tensor'=4] {'dp'}, dimensions={0}, use_global_device_ids=true | all-gather | bytes 746496 | tf_op jit(solution)/shard_map/all_gather | solution.py:626
  107.5 8.1 %add_convert_fusion.proj_ref = bf16[2,736,864]{2,1,0:T(8,128)(2,1)} fusion(f32[864]{0:T(1024)S(1)} %pad_maximum_fusion, bf16[2,736,1152]{2,1,0:T(8,128)(2,1)} %bitcast.79, bf16[1152,864]{1,0:T(8,128)(2,1)} %all-gather.6.cloned.1.call-done), kind=kOutput, calls=%fused_computation.13 | convolution fusion | flops 2932789248 | bytes 7929216 | tf_op jit(solution)/shard_map/isd,df->isf/dot_general | solution.py:648
  115.7 16.2 %attend_forward.1 = bf16[2,736,288]{2,1,0:T(8,128)(2,1)} custom-call(s32[2]{0:T(128)} %reduce_sum.27.lens_ref, bf16[2,736,864]{2,1,0:T(8,128)(2,1)} %add_convert_fusion.proj_ref), custom_call_target="tpu_custom_call" | custom-call | tf_op jit(solution)/shard_map/attend_forward/pallas_call | solution.py:100
  131.8 5.0 convolution_convert_fusion.1
  136.8 62.4 %middle_plane.1 = (f32[2,184,1152]{2,1,0:T(8,128)}, bf16[2,4,184,1152]{3,2,1,0:T(8,128)(2,1)}) custom-call(bf16[2,4,184,1152]{3,2,1,0:T(8,128)(2,1)} %bitcast.66, bf16[2,184,1152]{2,1,0:T(8,128)(2,1)} %x_ref.5, f32[1,1152]{1,0:T(1,128)} %reshape.98.bias_ref, f32[1,1152]{1,0:T(1,128)} %reshape.99.gain_ref, f32[1,1152]{1,0:T(1,128)} %reshape.100.shift_ref), custom_call_target="tpu_custom_call" | custom-call | tf_op jit(solution)/shard_map/middle_plane/pallas_call | solution.py:401
  199.2 0.0 all-gather.8.cloned.1.call-done
  199.3 0.0 copy-start.10
  199.3 10.1 %fusion.10 = f32[2,736,1076]{1,2,0:T(8,128)} fusion(bf16[2,736,1152]{2,1,0:T(8,128)(2,1)} %bitcast.77, bf16[1152,1076]{1,0:T(8,128)(2,1)} %all-gather.8.cloned.1.call-done), kind=kOutput, calls=%fused_computation.22 | convolution fusion | flops 3649241088 | bytes 12206080 | tf_op jit(solution)/shard_map/isd,df->isf/dot_general | solution.py:661
  209.4 11.6 %convolution_convert_fusion.2 = bf16[2,736,1152]{2,1,0:T(8,128)(2,1)} fusion(bf16[1152,1076]{1,0:T(8,128)(2,1)} %all-gather.4.cloned.1.call-done, f32[2,736,1076]{1,2,0:T(8,128)} %fusion.10, f32[1076]{0:T(1024)S(1)} %copy-done.10), kind=kOutput, calls=%fused_computation.16 | convolution fusion | flops 3666775552 | bytes 12210384 | tf_op jit(solution)/shard_map/isf,df->isd/dot_general | solution.py:669
  221.0 9.7 %fusion.21 = (f32[1076]{0:T(1024)S(1)}, bf16[2,736,1076]{1,2,0:T(8,128)(2,1)S(1)}) fusion(f32[2,736,1076]{1,2,0:T(8,128)S(1)} %copy-done.11, f32[1076]{0:T(1024)S(1)} %copy-done.10, bf16[2,736,1152]{2,1,0:T(8,128)(2,1)S(1)} %bitcast.76, bf16[1152,1076]{1,0:T(8,128)(2,1)S(1)} %copy-done.9), kind=kOutput, calls=%fused_computation.47 | convolution fusion | flops 3682501376 | bytes 15382432 | tf_op jit(solution)/shard_map/isd,df->isf/dot_general | solution.py:664
  230.8 6.9 %convolution_convert_fusion.3 = bf16[2,736,1152]{2,1,0:T(8,128)(2,1)} fusion(bf16[1152,1076]{1,0:T(8,128)(2,1)S(1)} %copy-done.8, bf16[2,736,1076]{1,2,0:T(8,128)(2,1)S(1)} %get-tuple-element.95), kind=kOutput, calls=%fused_computation.17 | convolution fusion | flops 3650936832 | bytes 9038336 | tf_op jit(solution)/shard_map/isf,df->isd/dot_general | solution.py:668
  237.6 0.0 copy-start
  237.6 91.5 %turn_plane.1 = (bf16[2,184,1152]{2,1,0:T(8,128)(2,1)}, f32[2,184,1152]{2,1,0:T(8,128)}, bf16[2,4,184,1152]{3,2,1,0:T(8,128)(2,1)}, f32[4,1152]{1,0:T(4,128)}) custom-call(bf16[2,4,184,1152]{3,2,1,0:T(8,128)(2,1)} %bitcast.69, bf16[2,4,184,1152]{3,2,1,0:T(8,128)(2,1)} %bitcast.68, f32[2,184,1152]{2,1,0:T(8,128)} %get-tuple-element.31.hidden_ref, ...), custom_call_target="tpu_custom_call" | custom-call | tf_op jit(solution)/shard_map/turn_plane/pallas_call | solution.py:467
  329.2 4.9 fusion.8
  334.1 0.0 reduce-scatter.7.cloned.1.call-update
  334.1 0.0 reduce-scatter.5.cloned.1.call-start
  334.2 3.3 convolution_convert_fusion.4
  337.5 1.7 copy.41.gmix_ref
  339.2 28.8 %attend_backward.1 = (bf16[2,736,864]{2,1,0:T(8,128)(2,1)}, f32[2,1,864]{2,1,0:T(1,128)}) custom-call(s32[2]{0:T(128)} %reduce_sum.27.lens_ref, bf16[2,736,864]{2,1,0:T(8,128)(2,1)} %add_convert_fusion.proj_ref, bf16[2,736,288]{2,1,0:T(8,128)(2,1)} %copy.41.gmix_ref), custom_call_target="tpu_custom_call" | custom-call | tf_op jit(solution)/shard_map/attend_backward/pallas_call | solution.py:167
  368.0 7.9 %bitcast_convert_fusion = bf16[1152,864]{1,0:T(8,128)(2,1)} fusion(bf16[2,736,1152]{2,1,0:T(8,128)(2,1)} %bitcast.80, bf16[2,736,864]{2,1,0:T(8,128)(2,1)} %get-tuple-element.34), kind=kOutput, calls=%fused_computation.18 | convolution fusion | flops 2931240960 | bytes 7925760 | tf_op jit(solution)/shard_map/isd,isf->df/dot_general | solution.py:692
  375.9 0.0 reduce-scatter.5.cloned.1.call-update
  375.9 11.9 %reduce-scatter.11.cloned.1.call-start = ((), (), s32[]{:S(2)}) async-start(), calls=%async_computation.10 | async-start | bytes 2985984 | tf_op jit(solution)/shard_map/reduce_scatter | solution.py:629
  387.8 10.8 %fusion.1 = bf16[1152,1076]{1,0:T(8,128)(2,1)} fusion(bf16[2,736,1152]{2,1,0:T(8,128)(2,1)} %bitcast.75, f32[2,736,1076]{1,2,0:T(8,128)} %fusion.10, f32[1076]{0:T(1024)S(1)} %copy-done.10), kind=kOutput, calls=%fused_computation.5 | convolution fusion | flops 3666319360 | bytes 12210384 | tf_op jit(solution)/shard_map/isd,isf->df/dot_general | solution.py:686
  398.6 0.0 reduce-scatter.11.cloned.1.call-update
  398.6 0.0 reduce-scatter.9.cloned.1.call-start
  398.7 9.4 %fusion = bf16[1152,1076]{1,0:T(8,128)(2,1)} fusion(bf16[2,736,1152]{2,1,0:T(8,128)(2,1)} %bitcast.78, bf16[2,736,1076]{1,2,0:T(8,128)(2,1)} %copy-done.12), kind=kOutput, calls=%fused_computation.4 | convolution fusion | flops 3650480640 | bytes 9038336 | tf_op jit(solution)/shard_map/isd,isf->df/dot_general | solution.py:685
  408.1 0.0 reduce-scatter.9.cloned.1.call-update
  408.1 0.1 fusion.20
  408.2 0.1 concatenate.11
  408.3 0.6 reshape.107.own_ref
  408.9 8.1 %convolution_convert_fusion = bf16[2,736,1152]{2,1,0:T(8,128)(2,1)} fusion(bf16[2,736,864]{2,1,0:T(8,128)(2,1)} %get-tuple-element.34, bf16[1152,864]{1,0:T(8,128)(2,1)} %all-gather.6.cloned.1.call-done), kind=kOutput, calls=%fused_computation.14 | convolution fusion | flops 2931941376 | bytes 7925760 | tf_op jit(solution)/shard_map/isf,df->isd/dot_general | solution.py:690
  417.0 34.1 %close_plane.1 = (f32[2,184,1152]{2,1,0:T(8,128)}, f32[2,1152]{1,0:T(2,128)}) custom-call(bf16[2,4,184,1152]{3,2,1,0:T(8,128)(2,1)} %bitcast.67, bf16[2,184,1152]{2,1,0:T(8,128)(2,1)} %x_ref.5, f32[2,184,1152]{2,1,0:T(8,128)} %get-tuple-element.35.ghid_ref, f32[1,1152]{1,0:T(1,128)} %reshape.92.gain_ref), custom_call_target="tpu_custom_call" | custom-call | tf_op jit(solution)/shard_map/close_plane/pallas_call | solution.py:512
  451.1 1.4 select_maximum_fusion.both_ref
  452.5 19.7 %small_sums.1 = (f32[8,1152]{1,0:T(8,128)}, f32[8,256]{1,0:T(8,128)}) custom-call(f32[8,1152]{1,0:T(8,128)} %select_maximum_fusion.both_ref, f32[8,256]{1,0:T(8,128)} %reshape.107.own_ref), custom_call_target="tpu_custom_call" | custom-call | tf_op jit(solution)/shard_map/small_sums/pallas_call | solution.py:567
  472.3 0.7 copy.46
  473.0 0.7 slice.49
  473.6 0.7 reshape.111
  474.3 1.7 slice_reduce_fusion
  476.0 1.6 convert_bitcast_fusion.1
  477.6 1.6 reshape.113
  479.2 0.9 copy.43
  480.1 1.9 convert_bitcast_fusion
  481.9 10.5 %reduce-scatter.9.cloned.1.call-done = bf16[144,1076]{1,0:T(8,128)(2,1)} async-done(((bf16[1152,1076]{1,0:T(8,128)(2,1)}), bf16[144,1076]{1,0:T(8,128)(2,1)}) %reduce-scatter.9.cloned.1.call-update) | async-done | bytes 309904 | tf_op jit(solution)/shard_map/reduce_scatter | solution.py:629
  492.5 1.9 convert_element_type.57
  494.3 0.9 copy.49
  495.2 1.2 copy.50
  (34 shorter events, 0.1 us)
Async XLA Ops:
  7.2 78.2 %copy-start.6 = (f32[2,288]{1,0:T(2,128)S(1)}, f32[2,288]{1,0:T(2,128)}, u32[]{:S(2)}) copy-start(f32[2,288]{1,0:T(2,128)} %param.20) | copy-start | bytes 6916
  7.2 78.3 %copy-start.3 = (bf16[288,144]{0,1:T(8,128)(2,1)S(1)}, bf16[288,144]{0,1:T(8,128)(2,1)}, u32[]{:S(2)}) copy-start(bf16[288,144]{0,1:T(8,128)(2,1)} %param.21) | copy-start | bytes 248836
  7.2 100.3 %all-gather.6.cloned.1.call-start = ((), (), s32[]{:S(2)}) async-start(), calls=%async_computation.5 | async-start | bytes 2322432 | tf_op jit(solution)/shard_map/all_gather | solution.py:626
  9.4 189.9 %all-gather.8.cloned.1.call-start = ((), (), s32[]{:S(2)}) async-start(), calls=%async_computation.6 | async-start | bytes 2985984 | tf_op jit(solution)/shard_map/all_gather | solution.py:626
  10.2 199.2 %all-gather.4.cloned.1.call-start = ((), (), s32[]{:S(2)}) async-start(), calls=%async_computation.4 | async-start | bytes 2985984 | tf_op jit(solution)/shard_map/all_gather | solution.py:626
  10.9 465.1 %reduce-scatter.7.cloned.1.call-start = ((), (), s32[]{:S(2)}) async-start(), calls=%async_computation.8 | async-start | bytes 995328 | tf_op jit(solution)/shard_map/reduce_scatter | solution.py:629
  199.3 10.1 %copy-start.10 = (f32[1076]{0:T(1024)S(1)}, f32[1076]{0:T(1024)}, u32[]{:S(2)}) copy-start(f32[1076]{0:T(1024)} %param.26) | copy-start | bytes 12916
  209.3 11.7 %copy-start.7 = (bf16[2,4,184,1152]{3,2,1,0:T(8,128)(2,1)S(1)}, bf16[2,4,184,1152]{3,2,1,0:T(8,128)(2,1)}, u32[]{:S(2)}) copy-start(bf16[2,4,184,1152]{3,2,1,0:T(8,128)(2,1)} %get-tuple-element.28) | copy-start | bytes 10174468
  209.3 11.7 %copy-start.9 = (bf16[1152,1076]{1,0:T(8,128)(2,1)S(1)}, bf16[1152,1076]{1,0:T(8,128)(2,1)}, u32[]{:S(2)}) copy-start(bf16[1152,1076]{1,0:T(8,128)(2,1)} %all-gather.4.cloned.1.call-done) | copy-start | bytes 7437316
  209.3 11.7 %copy-start.11 = (f32[2,736,1076]{1,2,0:T(8,128)S(1)}, f32[2,736,1076]{1,2,0:T(8,128)}, u32[]{:S(2)}) copy-start(f32[2,736,1076]{1,2,0:T(8,128)} %fusion.10) | copy-start | bytes 19006468
  221.0 9.7 %copy-start.8 = (bf16[1152,1076]{1,0:T(8,128)(2,1)S(1)}, bf16[1152,1076]{1,0:T(8,128)(2,1)}, u32[]{:S(2)}) copy-start(bf16[1152,1076]{1,0:T(8,128)(2,1)} %all-gather.8.cloned.1.call-done) | copy-start | bytes 7437316
  230.7 6.9 %copy-start.12 = (bf16[2,736,1076]{1,2,0:T(8,128)(2,1)}, bf16[2,736,1076]{1,2,0:T(8,128)(2,1)S(1)}, u32[]{:S(2)}) copy-start(bf16[2,736,1076]{1,2,0:T(8,128)(2,1)S(1)} %get-tuple-element.95) | copy-start | bytes 9503236
  237.6 91.5 %copy-start = (bf16[2,736,288]{2,1,0:T(8,128)(2,1)S(1)}, bf16[2,736,288]{2,1,0:T(8,128)(2,1)}, u32[]{:S(2)}) copy-start(bf16[2,736,288]{2,1,0:T(8,128)(2,1)} %attend_forward.1) | copy-start | bytes 2543620
  334.1 143.5 %reduce-scatter.5.cloned.1.call-start = ((), (), s32[]{:S(2)}) async-start(), calls=%async_computation.7 | async-start | bytes 2322432 | tf_op jit(solution)/shard_map/reduce_scatter | solution.py:629
  375.9 104.2 %reduce-scatter.11.cloned.1.call-start = ((), (), s32[]{:S(2)}) async-start(), calls=%async_computation.10 | async-start | bytes 2985984 | tf_op jit(solution)/shard_map/reduce_scatter | solution.py:629
  398.6 9.5 %copy-start.5 = (f32[2,1,864]{2,1,0:T(1,128)S(1)}, f32[2,1,864]{2,1,0:T(1,128)}, u32[]{:S(2)}) copy-start(f32[2,1,864]{2,1,0:T(1,128)} %get-tuple-element.39) | copy-start | bytes 20740
  398.6 93.8 %reduce-scatter.9.cloned.1.call-start = ((), (), s32[]{:S(2)}) async-start(), calls=%async_computation.9 | async-start | bytes 2985984 | tf_op jit(solution)/shard_map/reduce_scatter | solution.py:629
  417.0 34.1 %copy-start.4 = (f32[4,1152]{1,0:T(4,128)S(1)}, f32[4,1152]{1,0:T(4,128)}, u32[]{:S(2)}) copy-start(f32[4,1152]{1,0:T(4,128)} %get-tuple-element.37) | copy-start | bytes 55300
  451.1 43.2 %copy-start.2 = (bf16[2,184,1152]{2,1,0:T(8,128)(2,1)S(1)}, bf16[2,184,1152]{2,1,0:T(8,128)(2,1)}, u32[]{:S(2)}) copy-start(bf16[2,184,1152]{2,1,0:T(8,128)(2,1)} %get-tuple-element.112) | copy-start | bytes 2543620
  474.3 20.9 %copy-start.1 = (f32[2,184,1152]{2,1,0:T(8,128)S(1)}, f32[2,184,1152]{2,1,0:T(8,128)}, u32[]{:S(2)}) copy-start(f32[2,184,1152]{2,1,0:T(8,128)} %get-tuple-element.113) | copy-start | bytes 5087236
Sparse Core Ops, SparseCore 0:
  10.2 31.6 all-gather.5
  43.5 33.3 all-gather.7
  78.6 40.1 all-gather.3
  334.2 30.8 reduce-scatter.6
  376.0 34.7 reduce-scatter.4
  413.0 36.5 reduce-scatter.10
  451.9 40.5 reduce-scatter.8
